TPU v7x, 32 devices: a whole 2x2x4 slice. The times are simulated.
32 devices in a mesh: row: 4 (over z), col: 8 (over y, x, core).
Axes of the slice: x: 2, y: 2, z: 4, core: 2. Of those that a mesh axis runs over, the one named last changes fastest.
Arguments:
- front_matrix: bfloat16 [32768, 32768], P('row', 'col'), may hold values from -0.03125 to 0.03125
- right_random: bfloat16 [32768, 128], P(('col', 'row')), may hold values from -32 to 32
- left_random: bfloat16 [32768, 128], P(('row', 'col')), may hold values from -32 to 32
- row_basis: bfloat16 [32768, 384], P('row'), may hold values from -1 to 1, as said below
- column_basis: bfloat16 [32768, 384], P('col'), may hold values from -1 to 1, as said below
Outputs:
- row_samples: float32 [128, 32768], P('col', 'row')
- column_samples: float32 [128, 32768], P('row', 'col')
- row_spread: float32 [64], P('row')
- column_spread: float32 [64], P('col')
Inputs may be any that keep to these rules, and one draw needn't show every extreme that they name: Within each leaf node's 512 rows, the columns of row_basis are orthonormal up to their rounding to bfloat16. Within each leaf node's 512 rows, the columns of column_basis are orthonormal up to their rounding to bfloat16.
All inputs are finite; a program needn't handle non-finite values.
Results may differ from a plain program's by a relative error of at most 0.0003.
Values may be sent and summed in bfloat16 or wider, within the bound.
No kernel may reach another device: no remote copies, remote signals or barrier semaphores. Data moves between devices by JAX's collectives and lax.ppermute only.
A program may use at most 128 MiB of HBM per device.

v0:
```python
import jax
import jax.numpy as jnp
from jax import lax
from jax.sharding import PartitionSpec as P

SAMPLES = 128
EARLIER = 384
NODE = 512


def project_out(samples, basis):
    count = samples.shape[0]
    nodes = basis.shape[0] // NODE
    shaped = samples.reshape(count, nodes, NODE)
    stacked = basis.astype(jnp.float32).reshape(nodes, NODE, EARLIER)
    coeffs = jnp.einsum("knr,nre->kne", shaped, stacked, precision=lax.Precision.HIGHEST)
    correction = jnp.einsum("kne,nre->knr", coeffs, stacked, precision=lax.Precision.HIGHEST)
    cleaned = shaped - correction
    squares = jnp.sum(cleaned * cleaned, axis=(0, 2))
    return (cleaned.reshape(count, nodes * NODE), squares)


def shards(front_matrix, right_random, left_random, row_basis, column_basis):
    row_partial = jnp.einsum(
        "jc,ij->ci",
        lax.all_gather(right_random, "row", axis=0, tiled=True),
        front_matrix,
        preferred_element_type=jnp.float32,
    )
    column_partial = jnp.einsum(
        "ic,ij->cj",
        lax.all_gather(left_random, "col", axis=0, tiled=True),
        front_matrix,
        preferred_element_type=jnp.float32,
    )
    row_mine = lax.psum_scatter(row_partial, "col", scatter_dimension=0, tiled=True)
    column_mine = lax.psum_scatter(column_partial, "row", scatter_dimension=0, tiled=True)
    row_samples, row_partial_sq = project_out(row_mine, row_basis)
    column_samples, column_partial_sq = project_out(column_mine, column_basis)
    row_total_sq = lax.psum(row_partial_sq, "col")
    column_total_sq = lax.psum(column_partial_sq, "row")
    row_spread = jnp.sqrt(row_total_sq / (SAMPLES * NODE))
    column_spread = jnp.sqrt(column_total_sq / (SAMPLES * NODE))
    return (row_samples, column_samples, row_spread, column_spread)


def solution(mesh):
    in_specs = (
        P("row", "col"),
        P(("col", "row"), None),
        P(("row", "col"), None),
        P("row", None),
        P("col", None),
    )
    out_specs = (P("col", "row"), P("row", "col"), P("row"), P("col"))
    return jax.shard_map(shards, mesh=mesh, in_specs=in_specs, out_specs=out_specs, check_vma=False)
```

profile of v0, /device:TPU:0, one launch (start us, length us, event | category | flops | bytes accessed | tf_op | source)
XLA Modules:
  0.0 207.1 jit_solution(11374009316376437406)
XLA Ops:
  7.2 0.0 copy-start
  7.2 0.0 all-gather.3.cloned.1.call-start
  7.2 0.7 all-gather.3.cloned.1.call-update
  7.9 0.0 all-gather.5.cloned.1.call-start
  8.0 0.7 all-gather.5.cloned.1.call-update
  8.7 0.0 reduce-scatter.3.cloned.1.call-start
  8.7 31.6 %all-gather.3.cloned.1.call-done = bf16[4096,128]{1,0:T(8,128)(2,1)} async-done(((bf16[1024,128]{1,0:T(8,128)(2,1)}), bf16[4096,128]{1,0:T(8,128)(2,1)}) %all-gather.3.cloned.1.call-update) | async-done | bytes 1048592 | tf_op jit(solution)/shard_map/all_gather | solution.py:26
  40.3 29.5 %fusion.6 = f32[128,8192]{1,0:T(8,128)} fusion(bf16[4096,128]{1,0:T(8,128)(2,1)} %all-gather.3.cloned.1.call-done, bf16[8192,4096]{1,0:T(8,128)(2,1)} %param.5), kind=kOutput, calls=%fused_computation.14 | convolution fusion | flops 8589934592 | bytes 72351744 | tf_op jit(solution)/shard_map/jc,ij->ci/dot_general | solution.py:24
  69.8 0.0 reduce-scatter.3.cloned.1.call-update
  69.8 0.2 reduce-scatter.5.cloned.1.call-start
  70.1 0.0 all-gather.5.cloned.1.call-done
  70.1 27.7 %fusion.7 = f32[128,4096]{1,0:T(8,128)} fusion(bf16[8192,128]{1,0:T(8,128)(2,1)} %all-gather.5.cloned.1.call-done, bf16[8192,4096]{1,0:T(8,128)(2,1)} %param.5), kind=kOutput, calls=%fused_computation.15 | convolution fusion | flops 8589934592 | bytes 71303168 | tf_op jit(solution)/shard_map/ic,ij->cj/dot_general | solution.py:30
  97.7 0.0 reduce-scatter.5.cloned.1.call-update
  97.8 26.1 %reduce-scatter.3.cloned.1.call-done = f32[16,8192]{1,0:T(8,128)} async-done(((f32[128,8192]{1,0:T(8,128)}), f32[16,8192]{1,0:T(8,128)}) %reduce-scatter.3.cloned.1.call-update) | async-done | bytes 524304 | tf_op jit(solution)/shard_map/reduce_scatter | solution.py:36
  123.9 0.0 copy-start.2
  123.9 5.6 %convolution_bitcast_fusion.3 = f32[16,16,384]{2,0,1:T(8,128)S(1)} fusion(bf16[16,512,384]{2,1,0:T(8,128)(2,1)} %bitcast.40, f32[2,16,8,512]{3,2,1,0:T(8,128)} %bitcast.45), kind=kOutput, calls=%fused_computation.5 | convolution fusion | flops 603979776 | bytes 7208960 | tf_op jit(solution)/shard_map/knr,nre->kne/dot_general | solution.py:16
  129.5 0.0 copy-done.2
  129.5 7.2 %multiply_reduce_fusion.1 = (f32[16]{0:T(128)S(1)}, f32[16,16,512]{2,0,1:T(8,128)S(1)}) fusion(f32[16,16,384]{2,0,1:T(8,128)S(1)} %convolution_bitcast_fusion.3, bf16[16,512,384]{2,1,0:T(8,128)(2,1)} %bitcast.41, f32[2,16,8,512]{3,2,1,0:T(8,128)S(1)} %bitcast.46), kind=kOutput, calls=%fused_computation.9 | convolution fusion | flops 604372992 | bytes 7733312 | tf_op jit(solution)/shard_map/kne,nre->knr/dot_general | solution.py:17
  136.7 0.8 copy.17
  137.5 32.2 %reduce-scatter.5.cloned.1.call-done = f32[32,4096]{1,0:T(8,128)} async-done(((f32[128,4096]{1,0:T(8,128)}), f32[32,4096]{1,0:T(8,128)}) %reduce-scatter.5.cloned.1.call-update) | async-done | bytes 524304 | tf_op jit(solution)/shard_map/reduce_scatter | solution.py:37
  169.7 0.0 copy-done
  169.7 0.0 copy-start.1
  169.7 2.6 %convolution_bitcast_fusion.2 = f32[32,8,384]{2,0,1:T(8,128)S(1)} fusion(bf16[8,512,384]{2,1,0:T(8,128)(2,1)S(1)} %bitcast.38, f32[4,8,8,512]{3,2,1,0:T(8,128)} %bitcast.43), kind=kOutput, calls=%fused_computation.4 | convolution fusion | flops 603979776 | bytes 4063232 | tf_op jit(solution)/shard_map/knr,nre->kne/dot_general | solution.py:16
  172.3 0.0 copy-done.1
  172.4 3.0 %multiply_reduce_fusion = (f32[8]{0:T(128)S(1)}, f32[32,8,512]{2,0,1:T(8,128)S(1)}) fusion(f32[32,8,384]{2,0,1:T(8,128)S(1)} %convolution_bitcast_fusion.2, bf16[8,512,384]{2,1,0:T(8,128)(2,1)S(1)} %bitcast.39, f32[4,8,8,512]{3,2,1,0:T(8,128)S(1)} %bitcast.44), kind=kOutput, calls=%fused_computation.8 | convolution fusion | flops 604372992 | bytes 4587552 | tf_op jit(solution)/shard_map/kne,nre->knr/dot_general | solution.py:17
  175.4 0.8 copy.18
  176.2 13.2 %psum.14 = f32[16]{0:T(128)S(1)} all-reduce(f32[16]{0:T(128)S(1)} %get-tuple-element.4), channel_id=1, replica_groups=mesh['row'=4,'col'=8] {'col'}, use_global_device_ids=true, to_apply=%region_3.0 | all-reduce | flops 16 | bytes 128 | tf_op jit(solution)/shard_map/psum | solution.py:40
  189.4 0.5 multiply_sqrt_fusion.1
  189.9 10.2 %psum.15 = f32[8]{0:T(128)S(1)} all-reduce(f32[8]{0:T(128)S(1)} %get-tuple-element.6), channel_id=1, replica_groups=mesh['row'=4,'col'=8] {'row'}, use_global_device_ids=true, to_apply=%region_5.0 | all-reduce | flops 8 | bytes 64 | tf_op jit(solution)/shard_map/psum | solution.py:41
  200.1 0.5 multiply_sqrt_fusion
Async XLA Ops:
  7.2 162.6 %copy-start = (bf16[4096,384]{1,0:T(8,128)(2,1)S(1)}, bf16[4096,384]{1,0:T(8,128)(2,1)}, u32[]{:S(2)}) copy-start(bf16[4096,384]{1,0:T(8,128)(2,1)} %param.9) | copy-start | bytes 9437188
  7.2 33.1 %all-gather.3.cloned.1.call-start = ((), (), s32[]{:S(2)}) async-start(), calls=%async_computation.2 | async-start | bytes 1310720 | tf_op jit(solution)/shard_map/all_gather | solution.py:26
  7.9 62.2 %all-gather.5.cloned.1.call-start = ((), (), s32[]{:S(2)}) async-start(), calls=%async_computation.4 | async-start | bytes 2359296 | tf_op jit(solution)/shard_map/all_gather | solution.py:32
  8.7 115.2 %reduce-scatter.3.cloned.1.call-start = ((), (), s32[]{:S(2)}) async-start(), calls=%async_computation.3 | async-start | bytes 4718592 | tf_op jit(solution)/shard_map/reduce_scatter | solution.py:36
  69.8 99.9 %reduce-scatter.5.cloned.1.call-start = ((), (), s32[]{:S(2)}) async-start(), calls=%async_computation.5 | async-start | bytes 2621440 | tf_op jit(solution)/shard_map/reduce_scatter | solution.py:37
  123.9 5.6 %copy-start.2 = (f32[16,8192]{1,0:T(8,128)S(1)}, f32[16,8192]{1,0:T(8,128)}, u32[]{:S(2)}) copy-start(f32[16,8192]{1,0:T(8,128)} %reduce-scatter.3.cloned.1.call-done) | copy-start | bytes 1572868
  169.7 2.6 %copy-start.1 = (f32[32,4096]{1,0:T(8,128)S(1)}, f32[32,4096]{1,0:T(8,128)}, u32[]{:S(2)}) copy-start(f32[32,4096]{1,0:T(8,128)} %reduce-scatter.5.cloned.1.call-done) | copy-start | bytes 1572868
Sparse Core Ops, SparseCore 0:
  9.6 30.6 all-gather.2
  42.2 27.1 all-gather.4
  72.7 51.1 reduce-scatter.2
  126.1 43.6 reduce-scatter.4
where the time goes:
time: 207 us
  waiting for transfers between devices  91.3 us (44%)
  matrix products  75.6 us (37%)
  blocking collectives  23.4 us (11%)
  between operations  13.8 us (7%)
    reduce_scatter x1, waiting for transfers between devices, shards(): lax.psum_scatter(column_partial, 'row', scatter_dimension=0, tiled=True)  32.2 us
    all_gather x1, waiting for transfers between devices, shards(): lax.all_gather(right_random, 'row', axis=0, tiled=True)  31.6 us
    dot_general x1, matrix products, shards(): jnp.einsum('jc,ij->ci', lax.all_gather(right_random, 'row', axis=0, tiled...  29.5 us
    dot_general x1, matrix products, shards(): jnp.einsum('ic,ij->cj', lax.all_gather(left_random, 'col', axis=0, tiled=...  27.7 us
    reduce_scatter x1, waiting for transfers between devices, shards(): lax.psum_scatter(row_partial, 'col', scatter_dimension=0, tiled=True)  26.1 us
    psum x1, blocking collectives, shards(): row_total_sq = lax.psum(row_partial_sq, 'col')  13.2 us
    dot_general x2, matrix products, project_out(): jnp.einsum('kne,nre->knr', coeffs, stacked, precision=lax.Precision.HIGHEST)  10.2 us
    psum x1, blocking collectives, shards(): column_total_sq = lax.psum(column_partial_sq, 'row')  10.2 us
  transfers between devices with their start and end apart: 4, of which 3 were waited for; matrix products, arithmetic and copies ran while one was open for 34% of the time, Pallas kernels for 0%

commit v1 on v0

--- a/solution.py
+++ b/solution.py
@@ -2,6 +2,7 @@
 import jax.numpy as jnp
 from jax import lax
 from jax.sharding import PartitionSpec as P
+from jax.lax import axis_index, axis_size, ppermute
 
 SAMPLES = 128
 EARLIER = 384
@@ -21,11 +22,31 @@
 
 
 def shards(front_matrix, right_random, left_random, row_basis, column_basis):
-    row_partial = jnp.einsum(
-        "jc,ij->ci",
-        lax.all_gather(right_random, "row", axis=0, tiled=True),
-        front_matrix,
-        preferred_element_type=jnp.float32,
+
+    def close_sizes(local, shard_axis, array_here):
+        right_arr, local_next, v_next = (
+            axis_size(shard_axis),
+            axis_index(shard_axis),
+            local.shape[0],
+        )
+        found = list(map(lambda t: (t, (t + 1) % right_arr), range(right_arr)))
+        f_now, view_out = (local, None)
+        for at in [*range(right_arr)]:
+            y = ppermute(f_now, shard_axis, found) if at < right_arr - 1 else None
+            item_now = array_here(f_now, (local_next - at) % right_arr * v_next)
+            view_out = item_now if view_out is None else view_out + item_now
+            f_now = y
+        return view_out
+
+    row_partial = close_sizes(
+        right_random,
+        "row",
+        lambda own_block, offset: jnp.einsum(
+            "jc,ij->ci",
+            own_block,
+            lax.dynamic_slice_in_dim(front_matrix, offset, own_block.shape[0], axis=1),
+            preferred_element_type=jnp.float32,
+        ),
     )
     column_partial = jnp.einsum(
         "ic,ij->cj",

time: 207 us -> 182 us (0.88)
  waiting for transfers between devices: 91.3 us -> 29.7 us
  matrix products: 75.6 us -> 91.6 us
  local copies, waits for them, and re-layouts: 1.69 us -> 15.3 us
  starting transfers between devices: 0.34 us -> 6.71 us
    all_gather x1 -> x0, waiting for transfers between devices: 31.6 us -> none  [shards(): lax.all_gather(right_random, 'row', axis=0, tiled=True)]
    reduce_scatter x1 -> x0, waiting for transfers between devices: 26.1 us -> none  [shards(): lax.psum_scatter(row_partial, 'col', scatter_dimension=0, tiled=True)]
    reduce_scatter x1, waiting for transfers between devices: 32.2 us -> 6.49 us  [shards(): lax.psum_scatter(column_partial, 'row', scatter_dimension=0, tiled=True)]
    unnamed x4, waiting for transfers between devices: 1.41 us -> 23.2 us
    dot_general x1 -> x4, matrix products: 29.5 us -> 41.1 us  [shards(): jnp.einsum('jc,ij->ci', own_block, lax.dynamic_slice_in_dim(front_matrix,...]
    unnamed x6 -> x8, local copies, waits for them, and re-layouts: 0.02 us -> 9.13 us
    ppermute x0 -> x3, starting transfers between devices: none -> 6.37 us  [close_sizes(): y = ppermute(f_now, shard_axis, found) if at < right_arr - 1 else None]
    reshape x0 -> x1, local copies, waits for them, and re-layouts: none -> 3.5 us  [project_out(): shaped = samples.reshape(count, nodes, NODE)]
  transfers between devices with their start and end apart: 4 -> 6, of which waited for: 3 -> 2; matrix products, arithmetic and copies ran while one was open for 34% -> 56% of each run, Pallas kernels for 0% -> 0%
where the time goes in v1:
time: 182 us
  matrix products  91.6 us (50%)
  waiting for transfers between devices  29.7 us (16%)
  blocking collectives  23.7 us (13%)
  local copies, waits for them, and re-layouts  15.3 us (8%)
  between operations  13.8 us (8%)
  starting transfers between devices  6.71 us (4%)
    dot_general x4, matrix products, shards(): jnp.einsum('jc,ij->ci', own_block, lax.dynamic_slice_in_dim(front_matrix,...  41.1 us
    dot_general x1, matrix products, shards(): jnp.einsum('ic,ij->cj', lax.all_gather(left_random, 'col', axis=0, tiled=...  28.4 us
    unnamed x4, waiting for transfers between devices  23.2 us
    psum x1, blocking collectives, shards(): row_total_sq = lax.psum(row_partial_sq, 'col')  13.6 us
    dot_general x2, matrix products, project_out(): jnp.einsum('kne,nre->knr', coeffs, stacked, precision=lax.Precision.HIGHEST)  11.6 us
    dot_general x2, matrix products, project_out(): jnp.einsum('knr,nre->kne', shaped, stacked, precision=lax.Precision.HIGHEST)  10.5 us
    psum x1, blocking collectives, shards(): column_total_sq = lax.psum(column_partial_sq, 'row')  10.1 us
    unnamed x8, local copies, waits for them, and re-layouts  9.13 us
  transfers between devices with their start and end apart: 6, of which 2 were waited for; matrix products, arithmetic and copies ran while one was open for 56% of the time, Pallas kernels for 0%

profile of v1, /device:TPU:0, one launch (start us, length us, event | category | flops | bytes accessed | tf_op | source)
XLA Modules:
  0.0 181.9 jit_solution(6840211523511487224)
XLA Ops:
  7.2 0.0 copy-start
  7.2 0.0 all-gather.2.cloned.1.call-start
  7.2 0.7 all-gather.2.cloned.1.call-update
  7.9 0.0 reduce-scatter.7.cloned.1.call-start
  8.0 3.1 %collective-permute-start = (bf16[1024,128]{1,0:T(8,128)(2,1)}, bf16[1024,128]{1,0:T(8,128)(2,1)S(1)}, u32[]{:S(2)}, u32[]{:S(2)}) collective-permute-start(bf16[1024,128]{1,0:T(8,128)(2,1)} %param.6), channel_id=1, source_target_pairs={{0,8},{8,16},{16,24},{24,0},{1,9},{9,17},{17,25},{25,1},{2,10},{10... | collective-permute-start | bytes 786440 | tf_op jit(solution)/shard_map/ppermute | solution.py:35
  11.1 12.2 %fusion.6 = f32[8192,128]{1,0:T(8,128)} fusion(bf16[1024,128]{1,0:T(8,128)(2,1)} %param.6, bf16[8192,4096]{1,0:T(8,128)(2,1)} %param.5, s32[]{:T(128)S(6)} %select_n.32), kind=kOutput, calls=%fused_computation.6 | convolution fusion | flops 2147483648 | bytes 21233668 | tf_op jit(solution)/shard_map/jc,ij->ci/dot_general | solution.py:44
  23.3 0.0 collective-permute-done
  23.3 1.6 collective-permute-start.1
  24.9 10.1 %fusion.8 = f32[8192,128]{1,0:T(8,128)S(1)} fusion(f32[8192,128]{1,0:T(8,128)} %fusion.6, bf16[1024,128]{1,0:T(8,128)(2,1)S(1)} %collective-permute-done, bf16[8192,4096]{1,0:T(8,128)(2,1)} %param.5, s32[]{:T(128)S(6)} %select_n.34), kind=kOutput, calls=%fused_computation.8 | convolution fusion | flops 2148532224 | bytes 25427972 | tf_op jit(solution)/shard_map/jc,ij->ci/dot_general | solution.py:44
  35.0 0.0 collective-permute-done.1
  35.0 1.7 collective-permute-start.2
  36.7 8.3 %fusion.11 = f32[8192,128]{1,0:T(8,128)S(1)} fusion(f32[8192,128]{1,0:T(8,128)S(1)} %fusion.8, bf16[1024,128]{1,0:T(8,128)(2,1)S(1)} %collective-permute-done.1, bf16[8192,4096]{1,0:T(8,128)(2,1)} %param.5, s32[]{:T(128)S(6)} %select_n.36), kind=kOutput, calls=%fused_computation.9 | convolution fusion | flops 2148532224 | bytes 25427972 | tf_op jit(solution)/shard_map/jc,ij->ci/dot_general | solution.py:44
  44.9 0.0 collective-permute-done.2
  45.0 10.5 %fusion.17 = f32[128,8192]{0,1:T(8,128)} fusion(f32[8192,128]{1,0:T(8,128)S(1)} %fusion.11, bf16[1024,128]{1,0:T(8,128)(2,1)S(1)} %collective-permute-done.2, bf16[8192,4096]{1,0:T(8,128)(2,1)} %param.5, s32[]{:T(128)S(6)} %select_n.38), kind=kOutput, calls=%fused_computation.11 | convolution fusion | flops 2148532224 | bytes 25427972 | tf_op jit(solution)/shard_map/jc,ij->ci/dot_general | solution.py:44
  55.5 5.6 %copy.29 = f32[128,8192]{1,0:T(8,128)} copy(f32[128,8192]{0,1:T(8,128)} %fusion.17) | data formatting | bytes 8388608
  61.1 0.0 reduce-scatter.7.cloned.1.call-update
  61.1 0.3 reduce-scatter.5.cloned.1.call-start
  61.4 0.0 all-gather.2.cloned.1.call-done
  61.4 28.4 %fusion.28 = f32[128,4096]{1,0:T(8,128)} fusion(bf16[8192,128]{1,0:T(8,128)(2,1)} %all-gather.2.cloned.1.call-done, bf16[8192,4096]{1,0:T(8,128)(2,1)} %param.5), kind=kOutput, calls=%fused_computation.28 | convolution fusion | flops 8589934592 | bytes 71303168 | tf_op jit(solution)/shard_map/ic,ij->cj/dot_general | solution.py:51
  89.8 0.0 reduce-scatter.5.cloned.1.call-update
  89.8 22.5 %reduce-scatter.7.cloned.1.call-done = f32[16,8192]{1,0:T(8,128)} async-done(((f32[128,8192]{1,0:T(8,128)}), f32[16,8192]{1,0:T(8,128)}) %reduce-scatter.7.cloned.1.call-update) | async-done | bytes 524304
  112.3 3.5 %copy.30 = f32[16,8192]{0,1:T(8,128)} copy(f32[16,8192]{1,0:T(8,128)} %reduce-scatter.7.cloned.1.call-done) | data formatting | bytes 1048576
  115.8 3.5 %copy.21 = f32[16,16,512]{2,0,1:T(8,128)} copy(f32[16,16,512]{0,2,1:T(8,128)} %bitcast.42) | data formatting | bytes 1048576 | tf_op jit(solution)/shard_map/reshape | solution.py:15
  119.3 0.0 copy-start.2
  119.3 7.9 %convolution_bitcast_fusion.3 = f32[16,16,384]{2,0,1:T(8,128)S(1)} fusion(f32[16,16,512]{0,2,1:T(8,128)} %bitcast.43, bf16[16,512,384]{2,1,0:T(8,128)(2,1)} %bitcast.44), kind=kOutput, calls=%fused_computation.17 | convolution fusion | flops 603979776 | bytes 7208960 | tf_op jit(solution)/shard_map/knr,nre->kne/dot_general | solution.py:17
  127.2 0.0 copy-done.2
  127.2 8.6 %multiply_reduce_fusion.1 = (f32[16]{0:T(128)S(1)}, f32[16,16,512]{2,0,1:T(8,128)}) fusion(f32[16,16,512]{2,0,1:T(8,128)S(1)} %copy-done.2, f32[16,16,384]{2,0,1:T(8,128)S(1)} %convolution_bitcast_fusion.3, bf16[16,512,384]{2,1,0:T(8,128)(2,1)} %bitcast.45), kind=kOutput, calls=%fused_computation.20 | convolution fusion | flops 604372992 | bytes 7733312 | tf_op jit(solution)/shard_map/kne,nre->knr/dot_general | solution.py:18
  135.8 13.6 %psum.14 = f32[16]{0:T(128)S(1)} all-reduce(f32[16]{0:T(128)S(1)} %get-tuple-element.4), channel_id=1, replica_groups=mesh['row'=4,'col'=8] {'col'}, use_global_device_ids=true, to_apply=%region_3.4 | all-reduce | flops 16 | bytes 128 | tf_op jit(solution)/shard_map/psum | solution.py:61
  149.4 1.9 %copy.32 = f32[16,2,8,512]{3,2,0,1:T(8,128)} copy(f32[16,2,8,512]{3,2,1,0:T(8,128)} %bitcast.49) | data formatting | bytes 1048576 | tf_op jit(solution)/shard_map/reshape | solution.py:21
  151.3 0.5 multiply_sqrt_fusion.1
  151.8 6.5 %reduce-scatter.5.cloned.1.call-done = f32[32,4096]{1,0:T(8,128)} async-done(((f32[128,4096]{1,0:T(8,128)}), f32[32,4096]{1,0:T(8,128)}) %reduce-scatter.5.cloned.1.call-update) | async-done | bytes 524304 | tf_op jit(solution)/shard_map/reduce_scatter | solution.py:58
  158.3 0.0 copy-start.1
  158.3 0.0 copy-done
  158.3 2.6 %convolution_bitcast_fusion.2 = f32[32,8,384]{2,0,1:T(8,128)S(1)} fusion(bf16[8,512,384]{2,1,0:T(8,128)(2,1)S(1)} %bitcast.40, f32[4,8,8,512]{3,2,1,0:T(8,128)} %bitcast.47), kind=kOutput, calls=%fused_computation.16 | convolution fusion | flops 603979776 | bytes 4063232 | tf_op jit(solution)/shard_map/knr,nre->kne/dot_general | solution.py:17
  160.9 0.0 copy-done.1
  160.9 3.0 %multiply_reduce_fusion = (f32[8]{0:T(128)S(1)}, f32[32,8,512]{2,0,1:T(8,128)S(1)}) fusion(f32[32,8,384]{2,0,1:T(8,128)S(1)} %convolution_bitcast_fusion.2, bf16[8,512,384]{2,1,0:T(8,128)(2,1)S(1)} %bitcast.41, f32[4,8,8,512]{3,2,1,0:T(8,128)S(1)} %bitcast.48), kind=kOutput, calls=%fused_computation.19 | convolution fusion | flops 604372992 | bytes 4587552 | tf_op jit(solution)/shard_map/kne,nre->knr/dot_general | solution.py:18
  163.9 0.8 copy.33
  164.7 10.1 %psum.15 = f32[8]{0:T(128)S(1)} all-reduce(f32[8]{0:T(128)S(1)} %get-tuple-element.6), channel_id=1, replica_groups=mesh['row'=4,'col'=8] {'row'}, use_global_device_ids=true, to_apply=%region_5.6 | all-reduce | flops 8 | bytes 64 | tf_op jit(solution)/shard_map/psum | solution.py:62
  174.8 0.5 multiply_sqrt_fusion
Async XLA Ops:
  7.2 151.1 %copy-start = (bf16[4096,384]{1,0:T(8,128)(2,1)S(1)}, bf16[4096,384]{1,0:T(8,128)(2,1)}, u32[]{:S(2)}) copy-start(bf16[4096,384]{1,0:T(8,128)(2,1)} %param.9) | copy-start | bytes 9437188
  7.2 54.2 %all-gather.2.cloned.1.call-start = ((), (), s32[]{:S(2)}) async-start(), calls=%async_computation.2 | async-start | bytes 2359296 | tf_op jit(solution)/shard_map/all_gather | solution.py:53
  7.9 104.4 %reduce-scatter.7.cloned.1.call-start = ((), (), s32[]{:S(2)}) async-start(), calls=%async_computation.4 | async-start | bytes 4718592
  8.0 15.3 %collective-permute-start = (bf16[1024,128]{1,0:T(8,128)(2,1)}, bf16[1024,128]{1,0:T(8,128)(2,1)S(1)}, u32[]{:S(2)}, u32[]{:S(2)}) collective-permute-start(bf16[1024,128]{1,0:T(8,128)(2,1)} %param.6), channel_id=1, source_target_pairs={{0,8},{8,16},{16,24},{24,0},{1,9},{9,17},{17,25},{25,1},{2,10},{10... | collective-permute-start | bytes 786440 | tf_op jit(solution)/shard_map/ppermute | solution.py:35
  23.3 11.7 %collective-permute-start.1 = (bf16[1024,128]{1,0:T(8,128)(2,1)S(1)}, bf16[1024,128]{1,0:T(8,128)(2,1)S(1)}, u32[]{:S(2)}, u32[]{:S(2)}) collective-permute-start(bf16[1024,128]{1,0:T(8,128)(2,1)S(1)} %collective-permute-done), channel_id=1, source_target_pairs={{0,8},{8,16},{16,24},{24,0},{1,9},{9,17},{17,25},{25,1},{2,10},{10... | collective-permute-start | bytes 786440 | tf_op jit(solution)/shard_map/ppermute | solution.py:35
  35.0 10.0 %collective-permute-start.2 = (bf16[1024,128]{1,0:T(8,128)(2,1)S(1)}, bf16[1024,128]{1,0:T(8,128)(2,1)S(1)}, u32[]{:S(2)}, u32[]{:S(2)}) collective-permute-start(bf16[1024,128]{1,0:T(8,128)(2,1)S(1)} %collective-permute-done.1), channel_id=1, source_target_pairs={{0,8},{8,16},{16,24},{24,0},{1,9},{9,17},{17,25},{25,1},{2,10},{10... | collective-permute-start | bytes 786440 | tf_op jit(solution)/shard_map/ppermute | solution.py:35
  61.1 97.1 %reduce-scatter.5.cloned.1.call-start = ((), (), s32[]{:S(2)}) async-start(), calls=%async_computation.3 | async-start | bytes 2621440 | tf_op jit(solution)/shard_map/reduce_scatter | solution.py:58
  119.3 7.9 %copy-start.2 = (f32[16,16,512]{2,0,1:T(8,128)S(1)}, f32[16,16,512]{2,0,1:T(8,128)}, u32[]{:S(2)}) copy-start(f32[16,16,512]{2,0,1:T(8,128)} %copy.21) | copy-start | bytes 1572868
  158.3 2.6 %copy-start.1 = (f32[32,4096]{1,0:T(8,128)S(1)}, f32[32,4096]{1,0:T(8,128)}, u32[]{:S(2)}) copy-start(f32[32,4096]{1,0:T(8,128)} %reduce-scatter.5.cloned.1.call-done) | copy-start | bytes 1572868
Sparse Core Ops, SparseCore 0:
  9.9 30.4 all-gather.1
  61.2 51.0 reduce-scatter.6
  114.6 43.6 reduce-scatter.4
